TPU v7x, 256 devices: a whole 4x4x8 slice. The times are simulated.
256 devices in a mesh: row: 4 (over x), col: 2 (over core), dp: 32 (over z, y).
Axes of the slice: x: 4, y: 4, z: 8, core: 2. Of those that a mesh axis runs over, the one named last changes fastest.
Arguments:
- out_grad: bfloat16 [32, 128, 4096], P('dp', 'col', 'row'), may hold values from -6 to 6
- saved_hidden: bfloat16 [32, 128, 14336], P('dp', 'row', 'col'), may hold values from -6 to 6
- down_weight: bfloat16 [14336, 4096], P(('col', 'dp'), 'row'), may hold values from -0.046875 to 0.046875
Outputs:
- hidden_grad: bfloat16 [32, 128, 14336], P('dp', 'row', 'col')
- weight_grad: bfloat16 [14336, 4096], P(('col', 'dp'), 'row')
All inputs are finite; a program needn't handle non-finite values.
Results may differ from a plain program's by a relative error of at most 0.009.
Values may be sent and summed in bfloat16 or wider, within the bound.
No kernel may reach another device: no remote copies, remote signals or barrier semaphores. Data moves between devices by JAX's collectives and lax.ppermute only.
A program may use at most 64 MiB of HBM per device.

v0:
```python
import jax
import jax.numpy as jnp
from jax import lax
from jax.sharding import Mesh
from jax.sharding import PartitionSpec as P

DP = ("z", "y")
COL_DP = ("col", "z", "y")


def crossed(value, by):
    cores = lax.axis_size("col")
    return lax.ppermute(value, "col", [(i, (i + by) % cores) for i in range(cores)])


def traded(value, axis, second):
    cores, devices = lax.axis_size("col"), lax.axis_size(axis)
    first = axis == "row"
    number = lambda c, place: (place + c) % devices * cores + c if first else c * devices + (place + c) % devices
    pairs = []
    for c in range(cores):
        for place in range(devices):
            other = place + (1 if (place % 2 == 0) != second else -1)
            pairs.append((number(c, place), number(c, other)))
    return lax.ppermute(value, (axis, "col") if first else ("col", axis), pairs)


def place_on(axis):
    return (lax.axis_index(axis) - lax.axis_index("col")) % lax.axis_size(axis)


def paired(own, other, odd):
    both = jnp.stack([own, other])
    return jnp.where(odd, both[::-1], both)


def gathered_pairs(value, axis):
    devices = lax.axis_size(axis)
    place = place_on(axis)
    odd, number = place % 2, place // 2
    ahead = 2 * odd - 1
    pair = paired(value, traded(value, axis, False), odd == 1)
    out = [(number, pair)]
    for step in range(2, devices // 2 + 1):
        pair = traded(pair, axis, step % 2 == 0)
        distance = step // 2 * (1 if step % 2 == 0 else -1)
        out.append(((number + ahead * distance) % (devices // 2), pair))
    return out


def around(axis):
    devices, index = lax.axis_size(axis), lax.axis_index(axis)
    ahead = 2 * (place_on(axis) % 2) - 1
    return [(index + 2) % devices, (index + ahead) % devices, (index - ahead) % devices, index]


def quartered(value, axis):
    beside = traded(value, axis, False)
    behind = traded(value, axis, True)
    return [traded(beside, axis, True), behind, beside, value]


def summed(part, axis):
    f32, bf16 = jnp.float32, jnp.bfloat16
    passed_on = traded(part(0).astype(bf16), axis, True)
    kept = traded(part(1).astype(bf16), axis, True)
    partners = part(2).astype(f32) + passed_on.astype(f32)
    came = traded(partners.astype(bf16), axis, False)
    return part(3).astype(f32) + kept.astype(f32) + came.astype(f32)


def on_device(out_grad, saved_hidden, down_weight):
    rows, cols, zs, ys = (lax.axis_size(a) for a in ("row", "col", "z", "y"))
    col = lax.axis_index("col")
    grad, hidden = out_grad[0], saved_hidden[0]
    units, width = down_weight.shape
    tokens, wide = hidden.shape
    block = ys * units
    f32, bf16 = jnp.float32, jnp.bfloat16

    parts = quartered(down_weight, "y")
    weight = jnp.zeros((block, width), down_weight.dtype)
    for index, part in zip(around("y"), parts):
        weight = lax.dynamic_update_slice(weight, part, (index * units, 0))

    mine = jnp.swapaxes(hidden.reshape(tokens, zs, block), 0, 1)
    mine = lax.all_to_all(mine, "z", 0, 0, tiled=True).reshape(zs * tokens, block)

    own = jnp.zeros((zs, *grad.shape), grad.dtype)
    for number, pair in gathered_pairs(grad, "z"):
        for n in range(2):
            own = lax.dynamic_update_slice(own, pair[n][None], ((2 * number + n + col) % zs, 0, 0))
    other = crossed(own, 1)
    per_core = rows // cols
    by_row = lambda v: jnp.swapaxes(v.reshape(zs, per_core, tokens, width), 0, 1)
    halves = jnp.concatenate([by_row(own), by_row(other)])
    grads = [
        lax.dynamic_index_in_dim(halves, (index - per_core * col) % rows, 0, keepdims=False).reshape(-1, width)
        for index in around("row")
    ]

    parts = quartered(mine, "row")
    hiddens = jnp.concatenate(parts)

    partial = lambda k: lax.dot_general(grads[k], weight, (((1,), (1,)), ((), ())), preferred_element_type=f32)
    local = summed(partial, "row").astype(bf16).reshape(zs, tokens, block)
    returned = lax.all_to_all(local, "z", 0, 0, tiled=True)
    hidden_grad = jnp.swapaxes(returned, 0, 1).reshape(1, tokens, wide)

    factor = f32(1.0) / jnp.sqrt(f32(rows * tokens * zs * ys))
    total = lax.dot_general(
        hiddens, jnp.concatenate(grads), (((0,), (0,)), ((), ())), preferred_element_type=f32
    ).astype(bf16)
    indices = around("y")
    take = lambda k: lax.dynamic_slice_in_dim(total, indices[k] * units, units, 0)
    weight_grad = (summed(take, "y") * factor).astype(bf16)
    return (hidden_grad, weight_grad)


def solution(mesh):
    dp = mesh.shape["dp"]
    split = Mesh(
        mesh.devices.reshape(mesh.shape["row"], mesh.shape["col"], 8, dp // 8),
        ("row", "col", "z", "y"),
    )
    in_specs = (P(DP, "col", "row"), P(DP, "row", "col"), P(COL_DP, "row"))
    out_specs = (P(DP, "row", "col"), P(COL_DP, "row"))
    return jax.shard_map(on_device, mesh=split, in_specs=in_specs, out_specs=out_specs, check_vma=False)
```

profile of v0, /device:TPU:32, one launch (start us, length us, event | category | flops | bytes accessed | tf_op | source)
XLA Modules:
  0.0 111.6 jit_solution(322461316838791584)
XLA Ops:
  0.6 1.9 %collective-permute-start = (bf16[64,1024]{1,0:T(8,128)(2,1)}, bf16[64,1024]{1,0:T(8,128)(2,1)S(1)}, u32[]{:S(2)}, u32[]{:S(2)}) collective-permute-start(bf16[64,1024]{1,0:T(8,128)(2,1)} %bitcast.44), channel_id=1, source_target_pairs={{0,4},{4,0},{8,12},{12,8},{16,20},{20,16},{24,28},{28,24},{36,40},... | collective-permute-start | bytes 393224 | tf_op jit(solution)/shard_map/ppermute | solution.py:25
  2.5 1.1 copy.11
  3.6 0.8 copy.10
  4.4 9.3 %all-to-all-start.1 = ((bf16[8,32,896]{2,1,0:T(8,128)(2,1)}), bf16[8,32,896]{2,1,0:T(8,128)(2,1)S(1)}, u32[]{:S(2)}, u32[]{:S(2)}) async-start(bf16[8,32,896]{2,1,0:T(8,128)(2,1)} %copy.10), calls=%async_computation.1 | async-start | bytes 917504 | tf_op jit(solution)/shard_map/all_to_all | solution.py:87
  13.9 1.6 %collective-permute-start.1 = (bf16[2,64,1024]{2,1,0:T(8,128)(2,1)S(1)}, bf16[2,64,1024]{2,1,0:T(8,128)(2,1)S(1)}, u32[]{:S(2)}, u32[]{:S(2)}) collective-permute-start(bf16[2,64,1024]{2,1,0:T(8,128)(2,1)S(1)} %reverse_select_fusion), channel_id=1, source_target_pairs={{0,28},{4,8},{8,4},{12,16},{16,12},{20,24},{24,20},{28,0},{36,32},... | collective-permute-start | bytes 786440 | tf_op jit(solution)/shard_map/ppermute | solution.py:25
  15.6 12.6 %collective-permute-done.1 = bf16[2,64,1024]{2,1,0:T(8,128)(2,1)S(1)} collective-permute-done((bf16[2,64,1024]{2,1,0:T(8,128)(2,1)S(1)}, bf16[2,64,1024]{2,1,0:T(8,128)(2,1)S(1)}, u32[]{:S(2)}, u32[]{:S(2)}) %collective-permute-start.1) | collective-permute-done | bytes 262176 | tf_op jit(solution)/shard_map/ppermute | solution.py:25
  28.3 2.5 %collective-permute-start.2 = (bf16[2,64,1024]{2,1,0:T(8,128)(2,1)S(1)}, bf16[2,64,1024]{2,1,0:T(8,128)(2,1)S(1)}, u32[]{:S(2)}, u32[]{:S(2)}) collective-permute-start(bf16[2,64,1024]{2,1,0:T(8,128)(2,1)S(1)} %collective-permute-done.1), channel_id=1, source_target_pairs={{0,4},{4,0},{8,12},{12,8},{16,20},{20,16},{24,28},{28,24},{36,40},... | collective-permute-start | bytes 786440 | tf_op jit(solution)/shard_map/ppermute | solution.py:25
  30.8 4.3 %collective-permute-done.2 = bf16[2,64,1024]{2,1,0:T(8,128)(2,1)S(1)} collective-permute-done((bf16[2,64,1024]{2,1,0:T(8,128)(2,1)S(1)}, bf16[2,64,1024]{2,1,0:T(8,128)(2,1)S(1)}, u32[]{:S(2)}, u32[]{:S(2)}) %collective-permute-start.2) | collective-permute-done | bytes 262176 | tf_op jit(solution)/shard_map/ppermute | solution.py:25
  35.1 2.5 %collective-permute-start.3 = (bf16[2,64,1024]{2,1,0:T(8,128)(2,1)S(1)}, bf16[2,64,1024]{2,1,0:T(8,128)(2,1)S(1)}, u32[]{:S(2)}, u32[]{:S(2)}) collective-permute-start(bf16[2,64,1024]{2,1,0:T(8,128)(2,1)S(1)} %collective-permute-done.2), channel_id=1, source_target_pairs={{0,28},{4,8},{8,4},{12,16},{16,12},{20,24},{24,20},{28,0},{36,32},... | collective-permute-start | bytes 786440 | tf_op jit(solution)/shard_map/ppermute | solution.py:25
  37.7 4.3 %collective-permute-done.3 = bf16[2,64,1024]{2,1,0:T(8,128)(2,1)S(1)} collective-permute-done((bf16[2,64,1024]{2,1,0:T(8,128)(2,1)S(1)}, bf16[2,64,1024]{2,1,0:T(8,128)(2,1)S(1)}, u32[]{:S(2)}, u32[]{:S(2)}) %collective-permute-start.3) | collective-permute-done | bytes 262176 | tf_op jit(solution)/shard_map/ppermute | solution.py:25
  42.5 3.0 %collective-permute-start.7 = (bf16[224,1024]{1,0:T(8,128)(2,1)S(1)}, bf16[224,1024]{1,0:T(8,128)(2,1)}, u32[]{:S(2)}, u32[]{:S(2)}) collective-permute-start(bf16[224,1024]{1,0:T(8,128)(2,1)S(1)} %copy-done), channel_id=1, source_target_pairs={{0,3},{1,2},{2,1},{3,0},{33,32},{34,35},{35,34},{32,33},{4,7},{5,6... | collective-permute-start | bytes 1376264 | tf_op jit(solution)/shard_map/ppermute | solution.py:25
  45.5 1.5 %collective-permute-start.11 = (bf16[256,896]{1,0:T(8,128)(2,1)S(1)}, bf16[256,896]{1,0:T(8,128)(2,1)S(1)}, u32[]{:S(2)}, u32[]{:S(2)}) collective-permute-start(bf16[256,896]{1,0:T(8,128)(2,1)S(1)} %bitcast.41), channel_id=1, source_target_pairs={{0,64},{64,0},{128,192},{192,128},{96,160},{160,96},{224,32},{32,2... | collective-permute-start | bytes 1376264 | tf_op jit(solution)/shard_map/ppermute | solution.py:25
  47.0 5.1 %collective-permute-done.6 = bf16[224,1024]{1,0:T(8,128)(2,1)} collective-permute-done((bf16[224,1024]{1,0:T(8,128)(2,1)S(1)}, bf16[224,1024]{1,0:T(8,128)(2,1)}, u32[]{:S(2)}, u32[]{:S(2)}) %collective-permute-start.6) | collective-permute-done | bytes 458784 | tf_op jit(solution)/shard_map/ppermute | solution.py:25
  52.2 1.1 constant_dynamic-update-slice_fusion.3
  53.3 3.6 %collective-permute-done.7 = bf16[224,1024]{1,0:T(8,128)(2,1)} collective-permute-done((bf16[224,1024]{1,0:T(8,128)(2,1)S(1)}, bf16[224,1024]{1,0:T(8,128)(2,1)}, u32[]{:S(2)}, u32[]{:S(2)}) %collective-permute-start.7) | collective-permute-done | bytes 458784 | tf_op jit(solution)/shard_map/ppermute | solution.py:25
  56.9 1.0 constant_dynamic-update-slice_fusion.2
  58.1 0.8 fusion.25
  59.6 2.8 %collective-permute-start.9 = (bf16[256,896]{1,0:T(8,128)(2,1)S(1)}, bf16[256,896]{1,0:T(8,128)(2,1)S(1)}, u32[]{:S(2)}, u32[]{:S(2)}) collective-permute-start(bf16[256,896]{1,0:T(8,128)(2,1)S(1)} %convolution_convert_fusion), channel_id=1, source_target_pairs={{0,192},{64,128},{128,64},{192,0},{96,32},{160,224},{224,160},{32,... | collective-permute-start | bytes 1376264 | tf_op jit(solution)/shard_map/ppermute | solution.py:25
  63.0 2.8 %collective-permute-start.12 = (bf16[256,896]{1,0:T(8,128)(2,1)S(1)}, bf16[256,896]{1,0:T(8,128)(2,1)S(1)}, u32[]{:S(2)}, u32[]{:S(2)}) collective-permute-start(bf16[256,896]{1,0:T(8,128)(2,1)S(1)} %collective-permute-done.11), channel_id=1, source_target_pairs={{0,192},{64,128},{128,64},{192,0},{96,32},{160,224},{224,160},{32,... | collective-permute-start | bytes 1376264 | tf_op jit(solution)/shard_map/ppermute | solution.py:25
  67.0 2.4 %collective-permute-done.9 = bf16[256,896]{1,0:T(8,128)(2,1)S(1)} collective-permute-done((bf16[256,896]{1,0:T(8,128)(2,1)S(1)}, bf16[256,896]{1,0:T(8,128)(2,1)S(1)}, u32[]{:S(2)}, u32[]{:S(2)}) %collective-permute-start.9) | collective-permute-done | bytes 458784 | tf_op jit(solution)/shard_map/ppermute | solution.py:25
  69.4 0.7 fusion.21
  70.7 7.4 %collective-permute-done.13 = bf16[256,896]{1,0:T(8,128)(2,1)S(1)} collective-permute-done((bf16[256,896]{1,0:T(8,128)(2,1)S(1)}, bf16[256,896]{1,0:T(8,128)(2,1)S(1)}, u32[]{:S(2)}, u32[]{:S(2)}) %collective-permute-start.13) | collective-permute-done | bytes 458784 | tf_op jit(solution)/shard_map/ppermute | solution.py:25
  78.1 6.0 %collective-permute-done.12 = bf16[256,896]{1,0:T(8,128)(2,1)S(1)} collective-permute-done((bf16[256,896]{1,0:T(8,128)(2,1)S(1)}, bf16[256,896]{1,0:T(8,128)(2,1)S(1)}, u32[]{:S(2)}, u32[]{:S(2)}) %collective-permute-start.12) | collective-permute-done | bytes 458784 | tf_op jit(solution)/shard_map/ppermute | solution.py:25
  84.1 2.1 %fusion.15 = bf16[896,1024]{1,0:T(8,128)(2,1)S(1)} fusion(bf16[256,1024]{1,0:T(8,128)(2,1)S(1)} %bitcast.32, bf16[256,1024]{1,0:T(8,128)(2,1)S(1)} %bitcast.37, bf16[256,1024]{1,0:T(8,128)(2,1)S(1)} %bitcast.35, bf16[256,1024]{1,0:T(8,128)(2,1)S(1)} %bitcast.39, bf16[256,896]{1,0:T(8,128)(2,1)S(1)} %bitcast.43, ...), kind=kOutput, calls=%fused_computation.23 | convolution fusion | flops 1895694336 | bytes 5767168 | tf_op jit(solution)/shard_map/dot_general | solution.py:111
  86.7 3.0 %collective-permute-start.14 = (bf16[224,1024]{1,0:T(8,128)(2,1)S(1)}, bf16[224,1024]{1,0:T(8,128)(2,1)}, u32[]{:S(2)}, u32[]{:S(2)}) collective-permute-start(bf16[224,1024]{1,0:T(8,128)(2,1)S(1)} %get-tuple-element.6), channel_id=1, source_target_pairs={{0,3},{1,2},{2,1},{3,0},{33,32},{34,35},{35,34},{32,33},{4,7},{5,6... | collective-permute-start | bytes 1376264 | tf_op jit(solution)/shard_map/ppermute | solution.py:25
  89.7 1.6 %fusion.22 = bf16[256,896]{1,0:T(8,128)(2,1)} fusion(bf16[256,1024]{1,0:T(8,128)(2,1)S(1)} %bitcast.33, bf16[896,1024]{1,0:T(8,128)(2,1)S(1)} %constant_dynamic-update-slice_fusion, bf16[256,896]{1,0:T(8,128)(2,1)S(1)} %collective-permute-done.10, bf16[256,896]{1,0:T(8,128)(2,1)S(1)} %collective-permute-done.8), kind=kOutput, calls=%fused_computation.30 | convolution fusion | flops 470908928 | bytes 3735552 | tf_op jit(solution)/shard_map/dot_general | solution.py:105
  91.2 7.4 %all-to-all-start = ((bf16[8,32,896]{2,1,0:T(8,128)(2,1)}), bf16[8,32,896]{2,1,0:T(8,128)(2,1)S(1)}, u32[]{:S(2)}, u32[]{:S(2)}) async-start(bf16[8,32,896]{2,1,0:T(8,128)(2,1)} %bitcast.10), calls=%async_computation | async-start | bytes 917504 | tf_op jit(solution)/shard_map/all_to_all | solution.py:107
  98.6 1.2 %add_convert_fusion = bf16[224,1024]{1,0:T(8,128)(2,1)S(1)} fusion(bf16[224,1024]{1,0:T(8,128)(2,1)} %collective-permute-done.15, bf16[896,1024]{1,0:T(8,128)(2,1)S(1)} %fusion.15, s32[]{:T(128)S(6)} %select_n.219), kind=kLoop, calls=%fused_computation.32 | loop fusion | flops 917504 | bytes 1376260 | tf_op jit(solution)/shard_map/convert_element_type | solution.py:68
  99.9 3.4 %collective-permute-done.14 = bf16[224,1024]{1,0:T(8,128)(2,1)} collective-permute-done((bf16[224,1024]{1,0:T(8,128)(2,1)S(1)}, bf16[224,1024]{1,0:T(8,128)(2,1)}, u32[]{:S(2)}, u32[]{:S(2)}) %collective-permute-start.14) | collective-permute-done | bytes 458784 | tf_op jit(solution)/shard_map/ppermute | solution.py:25
  103.3 5.1 %collective-permute-done.16 = bf16[224,1024]{1,0:T(8,128)(2,1)S(1)} collective-permute-done((bf16[224,1024]{1,0:T(8,128)(2,1)S(1)}, bf16[224,1024]{1,0:T(8,128)(2,1)S(1)}, u32[]{:S(2)}, u32[]{:S(2)}) %collective-permute-start.16) | collective-permute-done | bytes 458784 | tf_op jit(solution)/shard_map/ppermute | solution.py:25
  108.4 2.0 %multiply_convert_fusion = bf16[224,1024]{1,0:T(8,128)(2,1)} fusion(bf16[224,1024]{1,0:T(8,128)(2,1)S(1)} %collective-permute-done.16, bf16[224,1024]{1,0:T(8,128)(2,1)} %collective-permute-done.14, bf16[896,1024]{1,0:T(8,128)(2,1)S(1)} %fusion.15, s32[]{:T(128)S(6)} %select_n.220), kind=kLoop, calls=%fused_computation.31 | loop fusion | flops 1605632 | bytes 1835012 | tf_op jit(solution)/shard_map/convert_element_type | solution.py:116
  110.6 1.0 reshape.42
  (39 shorter events, 4.9 us)
Async XLA Ops:
  0.6 13.2 %copy-start.1 = (bf16[1,64,1024]{2,1,0:T(8,128)(2,1)S(1)}, bf16[1,64,1024]{2,1,0:T(8,128)(2,1)}, u32[]{:S(2)}) copy-start(bf16[1,64,1024]{2,1,0:T(8,128)(2,1)} %param.3) | copy-start | bytes 393220
  0.6 13.1 %collective-permute-start = (bf16[64,1024]{1,0:T(8,128)(2,1)}, bf16[64,1024]{1,0:T(8,128)(2,1)S(1)}, u32[]{:S(2)}, u32[]{:S(2)}) collective-permute-start(bf16[64,1024]{1,0:T(8,128)(2,1)} %bitcast.44), channel_id=1, source_target_pairs={{0,4},{4,0},{8,12},{12,8},{16,20},{20,16},{24,28},{28,24},{36,40},... | collective-permute-start | bytes 393224 | tf_op jit(solution)/shard_map/ppermute | solution.py:25
  2.5 39.6 %collective-permute-start.5 = (bf16[224,1024]{1,0:T(8,128)(2,1)}, bf16[224,1024]{1,0:T(8,128)(2,1)S(1)}, u32[]{:S(2)}, u32[]{:S(2)}) collective-permute-start(bf16[224,1024]{1,0:T(8,128)(2,1)} %param.5), channel_id=1, source_target_pairs={{0,1},{1,0},{2,3},{3,2},{33,34},{34,33},{35,32},{32,35},{4,5},{5,4... | collective-permute-start | bytes 1376264 | tf_op jit(solution)/shard_map/ppermute | solution.py:25
  4.4 41.0 %all-to-all-start.1 = ((bf16[8,32,896]{2,1,0:T(8,128)(2,1)}), bf16[8,32,896]{2,1,0:T(8,128)(2,1)S(1)}, u32[]{:S(2)}, u32[]{:S(2)}) async-start(bf16[8,32,896]{2,1,0:T(8,128)(2,1)} %copy.10), calls=%async_computation.1 | async-start | bytes 917504 | tf_op jit(solution)/shard_map/all_to_all | solution.py:87
  13.8 28.7 %copy-start = (bf16[224,1024]{1,0:T(8,128)(2,1)S(1)}, bf16[224,1024]{1,0:T(8,128)(2,1)}, u32[]{:S(2)}) copy-start(bf16[224,1024]{1,0:T(8,128)(2,1)} %param.5) | copy-start | bytes 1376260
  13.9 14.4 %collective-permute-start.1 = (bf16[2,64,1024]{2,1,0:T(8,128)(2,1)S(1)}, bf16[2,64,1024]{2,1,0:T(8,128)(2,1)S(1)}, u32[]{:S(2)}, u32[]{:S(2)}) collective-permute-start(bf16[2,64,1024]{2,1,0:T(8,128)(2,1)S(1)} %reverse_select_fusion), channel_id=1, source_target_pairs={{0,28},{4,8},{8,4},{12,16},{16,12},{20,24},{24,20},{28,0},{36,32},... | collective-permute-start | bytes 786440 | tf_op jit(solution)/shard_map/ppermute | solution.py:25
  28.3 6.9 %collective-permute-start.2 = (bf16[2,64,1024]{2,1,0:T(8,128)(2,1)S(1)}, bf16[2,64,1024]{2,1,0:T(8,128)(2,1)S(1)}, u32[]{:S(2)}, u32[]{:S(2)}) collective-permute-start(bf16[2,64,1024]{2,1,0:T(8,128)(2,1)S(1)} %collective-permute-done.1), channel_id=1, source_target_pairs={{0,4},{4,0},{8,12},{12,8},{16,20},{20,16},{24,28},{28,24},{36,40},... | collective-permute-start | bytes 786440 | tf_op jit(solution)/shard_map/ppermute | solution.py:25
  35.1 6.9 %collective-permute-start.3 = (bf16[2,64,1024]{2,1,0:T(8,128)(2,1)S(1)}, bf16[2,64,1024]{2,1,0:T(8,128)(2,1)S(1)}, u32[]{:S(2)}, u32[]{:S(2)}) collective-permute-start(bf16[2,64,1024]{2,1,0:T(8,128)(2,1)S(1)} %collective-permute-done.2), channel_id=1, source_target_pairs={{0,28},{4,8},{8,4},{12,16},{16,12},{20,24},{24,20},{28,0},{36,32},... | collective-permute-start | bytes 786440 | tf_op jit(solution)/shard_map/ppermute | solution.py:25
  42.0 16.1 %collective-permute-start.4 = (bf16[8,64,1024]{2,1,0:T(8,128)(2,1)S(1)}, bf16[8,64,1024]{2,1,0:T(8,128)(2,1)S(1)}, u32[]{:S(2)}, u32[]{:S(2)}) collective-permute-start(bf16[8,64,1024]{2,1,0:T(8,128)(2,1)S(1)} %slice_dynamic-update-slice_fusion), channel_id=1, source_target_pairs={{0,32},{32,0},{1,33},{33,1},{2,34},{34,2},{3,35},{35,3},{4,36},{36... | collective-permute-start | bytes 3145736 | tf_op jit(solution)/shard_map/ppermute | solution.py:13
  42.1 9.9 %collective-permute-start.6 = (bf16[224,1024]{1,0:T(8,128)(2,1)S(1)}, bf16[224,1024]{1,0:T(8,128)(2,1)}, u32[]{:S(2)}, u32[]{:S(2)}) collective-permute-start(bf16[224,1024]{1,0:T(8,128)(2,1)S(1)} %collective-permute-done.5), channel_id=1, source_target_pairs={{0,3},{1,2},{2,1},{3,0},{33,32},{34,35},{35,34},{32,33},{4,7},{5,6... | collective-permute-start | bytes 1376264 | tf_op jit(solution)/shard_map/ppermute | solution.py:25
  42.5 14.4 %collective-permute-start.7 = (bf16[224,1024]{1,0:T(8,128)(2,1)S(1)}, bf16[224,1024]{1,0:T(8,128)(2,1)}, u32[]{:S(2)}, u32[]{:S(2)}) collective-permute-start(bf16[224,1024]{1,0:T(8,128)(2,1)S(1)} %copy-done), channel_id=1, source_target_pairs={{0,3},{1,2},{2,1},{3,0},{33,32},{34,35},{35,34},{32,33},{4,7},{5,6... | collective-permute-start | bytes 1376264 | tf_op jit(solution)/shard_map/ppermute | solution.py:25
  45.5 17.5 %collective-permute-start.11 = (bf16[256,896]{1,0:T(8,128)(2,1)S(1)}, bf16[256,896]{1,0:T(8,128)(2,1)S(1)}, u32[]{:S(2)}, u32[]{:S(2)}) collective-permute-start(bf16[256,896]{1,0:T(8,128)(2,1)S(1)} %bitcast.41), channel_id=1, source_target_pairs={{0,64},{64,0},{128,192},{192,128},{96,160},{160,96},{224,32},{32,2... | collective-permute-start | bytes 1376264 | tf_op jit(solution)/shard_map/ppermute | solution.py:25
  59.6 9.8 %collective-permute-start.9 = (bf16[256,896]{1,0:T(8,128)(2,1)S(1)}, bf16[256,896]{1,0:T(8,128)(2,1)S(1)}, u32[]{:S(2)}, u32[]{:S(2)}) collective-permute-start(bf16[256,896]{1,0:T(8,128)(2,1)S(1)} %convolution_convert_fusion), channel_id=1, source_target_pairs={{0,192},{64,128},{128,64},{192,0},{96,32},{160,224},{224,160},{32,... | collective-permute-start | bytes 1376264 | tf_op jit(solution)/shard_map/ppermute | solution.py:25
  62.5 15.7 %collective-permute-start.13 = (bf16[256,896]{1,0:T(8,128)(2,1)S(1)}, bf16[256,896]{1,0:T(8,128)(2,1)S(1)}, u32[]{:S(2)}, u32[]{:S(2)}) collective-permute-start(bf16[256,896]{1,0:T(8,128)(2,1)S(1)} %bitcast.42), channel_id=1, source_target_pairs={{0,192},{64,128},{128,64},{192,0},{96,32},{160,224},{224,160},{32,... | collective-permute-start | bytes 1376264 | tf_op jit(solution)/shard_map/ppermute | solution.py:25
  63.0 21.2 %collective-permute-start.12 = (bf16[256,896]{1,0:T(8,128)(2,1)S(1)}, bf16[256,896]{1,0:T(8,128)(2,1)S(1)}, u32[]{:S(2)}, u32[]{:S(2)}) collective-permute-start(bf16[256,896]{1,0:T(8,128)(2,1)S(1)} %collective-permute-done.11), channel_id=1, source_target_pairs={{0,192},{64,128},{128,64},{192,0},{96,32},{160,224},{224,160},{32,... | collective-permute-start | bytes 1376264 | tf_op jit(solution)/shard_map/ppermute | solution.py:25
  66.5 23.2 %collective-permute-start.8 = (bf16[256,896]{1,0:T(8,128)(2,1)S(1)}, bf16[256,896]{1,0:T(8,128)(2,1)S(1)}, u32[]{:S(2)}, u32[]{:S(2)}) collective-permute-start(bf16[256,896]{1,0:T(8,128)(2,1)S(1)} %convolution_convert_fusion.1), channel_id=1, source_target_pairs={{0,192},{64,128},{128,64},{192,0},{96,32},{160,224},{224,160},{32,... | collective-permute-start | bytes 1376264 | tf_op jit(solution)/shard_map/ppermute | solution.py:25
  70.2 19.5 %collective-permute-start.10 = (bf16[256,896]{1,0:T(8,128)(2,1)S(1)}, bf16[256,896]{1,0:T(8,128)(2,1)S(1)}, u32[]{:S(2)}, u32[]{:S(2)}) collective-permute-start(bf16[256,896]{1,0:T(8,128)(2,1)S(1)} %fusion.21), channel_id=1, source_target_pairs={{0,64},{64,0},{128,192},{192,128},{96,160},{160,96},{224,32},{32,2... | collective-permute-start | bytes 1376264 | tf_op jit(solution)/shard_map/ppermute | solution.py:25
  86.3 12.3 %collective-permute-start.15 = (bf16[224,1024]{1,0:T(8,128)(2,1)S(1)}, bf16[224,1024]{1,0:T(8,128)(2,1)}, u32[]{:S(2)}, u32[]{:S(2)}) collective-permute-start(bf16[224,1024]{1,0:T(8,128)(2,1)S(1)} %get-tuple-element.7), channel_id=1, source_target_pairs={{0,3},{1,2},{2,1},{3,0},{33,32},{34,35},{35,34},{32,33},{4,7},{5,6... | collective-permute-start | bytes 1376264 | tf_op jit(solution)/shard_map/ppermute | solution.py:25
  86.7 16.6 %collective-permute-start.14 = (bf16[224,1024]{1,0:T(8,128)(2,1)S(1)}, bf16[224,1024]{1,0:T(8,128)(2,1)}, u32[]{:S(2)}, u32[]{:S(2)}) collective-permute-start(bf16[224,1024]{1,0:T(8,128)(2,1)S(1)} %get-tuple-element.6), channel_id=1, source_target_pairs={{0,3},{1,2},{2,1},{3,0},{33,32},{34,35},{35,34},{32,33},{4,7},{5,6... | collective-permute-start | bytes 1376264 | tf_op jit(solution)/shard_map/ppermute | solution.py:25
  91.2 19.2 %all-to-all-start = ((bf16[8,32,896]{2,1,0:T(8,128)(2,1)}), bf16[8,32,896]{2,1,0:T(8,128)(2,1)S(1)}, u32[]{:S(2)}, u32[]{:S(2)}) async-start(bf16[8,32,896]{2,1,0:T(8,128)(2,1)} %bitcast.10), calls=%async_computation | async-start | bytes 917504 | tf_op jit(solution)/shard_map/all_to_all | solution.py:107
  99.8 8.6 %collective-permute-start.16 = (bf16[224,1024]{1,0:T(8,128)(2,1)S(1)}, bf16[224,1024]{1,0:T(8,128)(2,1)S(1)}, u32[]{:S(2)}, u32[]{:S(2)}) collective-permute-start(bf16[224,1024]{1,0:T(8,128)(2,1)S(1)} %add_convert_fusion), channel_id=1, source_target_pairs={{0,1},{1,0},{2,3},{3,2},{33,34},{34,33},{35,32},{32,35},{4,5},{5,4... | collective-permute-start | bytes 1376264 | tf_op jit(solution)/shard_map/ppermute | solution.py:25
where the time goes:
time: 113 us; the launch traced here: 112 us
  waiting for transfers between devices  54.3 us (48%)
  starting transfers between devices  40.7 us (36%)
  matrix products  5.9 us (5%)
  local copies, waits for them, and re-layouts  5.73 us (5%)
  other arithmetic  4.06 us (4%)
    ppermute x16, waiting for transfers between devices, traded(): return lax.ppermute(value, (axis, 'col') if first else ('col', axis), pairs)  54.3 us
    ppermute x16, starting transfers between devices, traded(): return lax.ppermute(value, (axis, 'col') if first else ('col', axis), pairs)  23.9 us
    all_to_all x1, starting transfers between devices, on_device(): lax.all_to_all(mine, 'z', 0, 0, tiled=True).reshape(zs * tokens, block)  9.34 us
    all_to_all x1, starting transfers between devices, on_device(): returned = lax.all_to_all(local, 'z', 0, 0, tiled=True)  7.42 us
    dot_general x4, matrix products, on_device(): lax.dot_general(grads[k], weight, (((1,), (1,)), ((), ())), preferred_ele...  3.79 us
  transfers between devices with their start and end apart: 19, of which 10 were waited for; matrix products, arithmetic and copies ran while one was open for 13% of the time, Pallas kernels for 0%

commit v1 on v0

--- a/solution.py
+++ b/solution.py
@@ -60,13 +60,17 @@
     return [traded(beside, axis, True), behind, beside, value]
 
 
-def summed(part, axis):
+def summed(part, axis, early):
     f32, bf16 = jnp.float32, jnp.bfloat16
-    passed_on = traded(part(0).astype(bf16), axis, True)
-    kept = traded(part(1).astype(bf16), axis, True)
-    partners = part(2).astype(f32) + passed_on.astype(f32)
+    first, second = part(0).astype(bf16), part(1).astype(bf16)
+    third, fourth = part(2).astype(f32), part(3).astype(f32)
+    if early:
+        third, fourth = lax.optimization_barrier((third, fourth))
+    passed_on = traded(first, axis, True)
+    kept = traded(second, axis, True)
+    partners = third + passed_on.astype(f32)
     came = traded(partners.astype(bf16), axis, False)
-    return part(3).astype(f32) + kept.astype(f32) + came.astype(f32)
+    return fourth + kept.astype(f32) + came.astype(f32)
 
 
 def on_device(out_grad, saved_hidden, down_weight):
@@ -103,7 +107,7 @@
     hiddens = jnp.concatenate(parts)
 
     partial = lambda k: lax.dot_general(grads[k], weight, (((1,), (1,)), ((), ())), preferred_element_type=f32)
-    local = summed(partial, "row").astype(bf16).reshape(zs, tokens, block)
+    local = summed(partial, "row", True).astype(bf16).reshape(zs, tokens, block)
     returned = lax.all_to_all(local, "z", 0, 0, tiled=True)
     hidden_grad = jnp.swapaxes(returned, 0, 1).reshape(1, tokens, wide)
 
@@ -113,7 +117,7 @@
     ).astype(bf16)
     indices = around("y")
     take = lambda k: lax.dynamic_slice_in_dim(total, indices[k] * units, units, 0)
-    weight_grad = (summed(take, "y") * factor).astype(bf16)
+    weight_grad = (summed(take, "y", False) * factor).astype(bf16)
     return (hidden_grad, weight_grad)
 
 

time: 113 us -> 110 us (0.973)
  the two profiles are of different devices: /device:TPU:32 before, /device:TPU:1 now
where the time goes in v1:
time: 110 us
  waiting for transfers between devices  57.3 us (52%)
  starting transfers between devices  35.6 us (32%)
  local copies, waits for them, and re-layouts  5.73 us (5%)
  matrix products  5.08 us (5%)
  other arithmetic  5.04 us (5%)
  between operations  1.16 us (1%)
    ppermute x16, waiting for transfers between devices, traded(): return lax.ppermute(value, (axis, 'col') if first else ('col', axis), pairs)  52.9 us
    ppermute x16, starting transfers between devices, traded(): return lax.ppermute(value, (axis, 'col') if first else ('col', axis), pairs)  23.8 us
    all_to_all x1, starting transfers between devices, on_device(): returned = lax.all_to_all(local, 'z', 0, 0, tiled=True)  4.4 us
    all_to_all x1, waiting for transfers between devices, on_device(): returned = lax.all_to_all(local, 'z', 0, 0, tiled=True)  4.4 us
    ppermute x1, starting transfers between devices, crossed(): lax.ppermute(value, 'col', [(i, (i + by) % cores) for i in range(cores)])  3.86 us
    all_to_all x1, starting transfers between devices, on_device(): lax.all_to_all(mine, 'z', 0, 0, tiled=True).reshape(zs * tokens, block)  3.47 us
    dot_general x4, matrix products, on_device(): lax.dot_general(grads[k], weight, (((1,), (1,)), ((), ())), preferred_ele...  2.97 us
  transfers between devices with their start and end apart: 19, of which 9 were waited for; matrix products, arithmetic and copies ran while one was open for 13% of the time, Pallas kernels for 0%

profile of v1, /device:TPU:1, one launch (start us, length us, event | category | flops | bytes accessed | tf_op | source)
XLA Modules:
  0.0 109.9 jit_solution(17903497602714442530)
XLA Ops:
  0.6 6.5 %collective-permute-start = (bf16[64,1024]{1,0:T(8,128)(2,1)}, bf16[64,1024]{1,0:T(8,128)(2,1)S(1)}, u32[]{:S(2)}, u32[]{:S(2)}) collective-permute-start(bf16[64,1024]{1,0:T(8,128)(2,1)} %bitcast.44), channel_id=1, source_target_pairs={{0,4},{4,0},{8,12},{12,8},{16,20},{20,16},{24,28},{28,24},{36,40},... | collective-permute-start | bytes 393224 | tf_op jit(solution)/shard_map/ppermute | solution.py:25
  7.1 2.7 %collective-permute-start.5 = (bf16[224,1024]{1,0:T(8,128)(2,1)}, bf16[224,1024]{1,0:T(8,128)(2,1)S(1)}, u32[]{:S(2)}, u32[]{:S(2)}) collective-permute-start(bf16[224,1024]{1,0:T(8,128)(2,1)} %param.5), channel_id=1, source_target_pairs={{0,1},{1,0},{2,3},{3,2},{33,34},{34,33},{35,32},{32,35},{4,5},{5,4... | collective-permute-start | bytes 1376264 | tf_op jit(solution)/shard_map/ppermute | solution.py:25
  9.9 1.1 copy.11
  10.9 0.8 copy.10
  11.7 3.5 %all-to-all-start.1 = ((bf16[8,32,896]{2,1,0:T(8,128)(2,1)}), bf16[8,32,896]{2,1,0:T(8,128)(2,1)S(1)}, u32[]{:S(2)}, u32[]{:S(2)}) async-start(bf16[8,32,896]{2,1,0:T(8,128)(2,1)} %copy.10), calls=%async_computation.1 | async-start | bytes 917504 | tf_op jit(solution)/shard_map/all_to_all | solution.py:91
  15.6 1.2 %collective-permute-start.1 = (bf16[2,64,1024]{2,1,0:T(8,128)(2,1)S(1)}, bf16[2,64,1024]{2,1,0:T(8,128)(2,1)S(1)}, u32[]{:S(2)}, u32[]{:S(2)}) collective-permute-start(bf16[2,64,1024]{2,1,0:T(8,128)(2,1)S(1)} %reverse_select_fusion), channel_id=1, source_target_pairs={{0,28},{4,8},{8,4},{12,16},{16,12},{20,24},{24,20},{28,0},{36,32},... | collective-permute-start | bytes 786440 | tf_op jit(solution)/shard_map/ppermute | solution.py:25
  17.0 13.7 %collective-permute-done.1 = bf16[2,64,1024]{2,1,0:T(8,128)(2,1)S(1)} collective-permute-done((bf16[2,64,1024]{2,1,0:T(8,128)(2,1)S(1)}, bf16[2,64,1024]{2,1,0:T(8,128)(2,1)S(1)}, u32[]{:S(2)}, u32[]{:S(2)}) %collective-permute-start.1) | collective-permute-done | bytes 262176 | tf_op jit(solution)/shard_map/ppermute | solution.py:25
  30.7 2.2 %collective-permute-start.2 = (bf16[2,64,1024]{2,1,0:T(8,128)(2,1)S(1)}, bf16[2,64,1024]{2,1,0:T(8,128)(2,1)S(1)}, u32[]{:S(2)}, u32[]{:S(2)}) collective-permute-start(bf16[2,64,1024]{2,1,0:T(8,128)(2,1)S(1)} %collective-permute-done.1), channel_id=1, source_target_pairs={{0,4},{4,0},{8,12},{12,8},{16,20},{20,16},{24,28},{28,24},{36,40},... | collective-permute-start | bytes 786440 | tf_op jit(solution)/shard_map/ppermute | solution.py:25
  32.9 4.2 %collective-permute-done.2 = bf16[2,64,1024]{2,1,0:T(8,128)(2,1)S(1)} collective-permute-done((bf16[2,64,1024]{2,1,0:T(8,128)(2,1)S(1)}, bf16[2,64,1024]{2,1,0:T(8,128)(2,1)S(1)}, u32[]{:S(2)}, u32[]{:S(2)}) %collective-permute-start.2) | collective-permute-done | bytes 262176 | tf_op jit(solution)/shard_map/ppermute | solution.py:25
  37.2 5.2 %collective-permute-done.3 = bf16[2,64,1024]{2,1,0:T(8,128)(2,1)S(1)} collective-permute-done((bf16[2,64,1024]{2,1,0:T(8,128)(2,1)S(1)}, bf16[2,64,1024]{2,1,0:T(8,128)(2,1)S(1)}, u32[]{:S(2)}, u32[]{:S(2)}) %collective-permute-start.3) | collective-permute-done | bytes 262176 | tf_op jit(solution)/shard_map/ppermute | solution.py:25
  42.4 3.9 %collective-permute-start.4 = (bf16[8,64,1024]{2,1,0:T(8,128)(2,1)S(1)}, bf16[8,64,1024]{2,1,0:T(8,128)(2,1)S(1)}, u32[]{:S(2)}, u32[]{:S(2)}) collective-permute-start(bf16[8,64,1024]{2,1,0:T(8,128)(2,1)S(1)} %slice_dynamic-update-slice_fusion), channel_id=1, source_target_pairs={{0,32},{32,0},{1,33},{33,1},{2,34},{34,2},{3,35},{35,3},{4,36},{36... | collective-permute-start | bytes 3145736 | tf_op jit(solution)/shard_map/ppermute | solution.py:13
  46.2 1.5 %collective-permute-start.7 = (bf16[224,1024]{1,0:T(8,128)(2,1)S(1)}, bf16[224,1024]{1,0:T(8,128)(2,1)}, u32[]{:S(2)}, u32[]{:S(2)}) collective-permute-start(bf16[224,1024]{1,0:T(8,128)(2,1)S(1)} %copy-done), channel_id=1, source_target_pairs={{0,3},{1,2},{2,1},{3,0},{33,32},{34,35},{35,34},{32,33},{4,7},{5,6... | collective-permute-start | bytes 1376264 | tf_op jit(solution)/shard_map/ppermute | solution.py:25
  47.7 2.5 %collective-permute-start.11 = (bf16[256,896]{1,0:T(8,128)(2,1)S(1)}, bf16[256,896]{1,0:T(8,128)(2,1)S(1)}, u32[]{:S(2)}, u32[]{:S(2)}) collective-permute-start(bf16[256,896]{1,0:T(8,128)(2,1)S(1)} %bitcast.41), channel_id=1, source_target_pairs={{0,64},{64,0},{128,192},{192,128},{96,160},{160,96},{224,32},{32,2... | collective-permute-start | bytes 1376264 | tf_op jit(solution)/shard_map/ppermute | solution.py:25
  50.2 3.8 %collective-permute-done.6 = bf16[224,1024]{1,0:T(8,128)(2,1)} collective-permute-done((bf16[224,1024]{1,0:T(8,128)(2,1)S(1)}, bf16[224,1024]{1,0:T(8,128)(2,1)}, u32[]{:S(2)}, u32[]{:S(2)}) %collective-permute-start.6) | collective-permute-done | bytes 458784 | tf_op jit(solution)/shard_map/ppermute | solution.py:25
  54.2 1.1 constant_dynamic-update-slice_fusion.3
  55.3 3.6 %collective-permute-done.7 = bf16[224,1024]{1,0:T(8,128)(2,1)} collective-permute-done((bf16[224,1024]{1,0:T(8,128)(2,1)S(1)}, bf16[224,1024]{1,0:T(8,128)(2,1)}, u32[]{:S(2)}, u32[]{:S(2)}) %collective-permute-start.7) | collective-permute-done | bytes 458784 | tf_op jit(solution)/shard_map/ppermute | solution.py:25
  58.9 1.0 constant_dynamic-update-slice_fusion.2
  60.1 1.3 %collective-permute-start.12 = (bf16[256,896]{1,0:T(8,128)(2,1)S(1)}, bf16[256,896]{1,0:T(8,128)(2,1)S(1)}, u32[]{:S(2)}, u32[]{:S(2)}) collective-permute-start(bf16[256,896]{1,0:T(8,128)(2,1)S(1)} %collective-permute-done.11), channel_id=1, source_target_pairs={{0,192},{64,128},{128,64},{192,0},{96,32},{160,224},{224,160},{32,... | collective-permute-start | bytes 1376264 | tf_op jit(solution)/shard_map/ppermute | solution.py:25
  61.4 0.8 fusion.23
  65.5 1.3 %collective-permute-start.8 = (bf16[256,896]{1,0:T(8,128)(2,1)S(1)}, bf16[256,896]{1,0:T(8,128)(2,1)S(1)}, u32[]{:S(2)}, u32[]{:S(2)}) collective-permute-start(bf16[256,896]{1,0:T(8,128)(2,1)S(1)} %convolution_convert_fusion.1), channel_id=1, source_target_pairs={{0,192},{64,128},{128,64},{192,0},{96,32},{160,224},{224,160},{32,... | collective-permute-start | bytes 1376264 | tf_op jit(solution)/shard_map/ppermute | solution.py:25
  66.8 5.9 %collective-permute-done.9 = bf16[256,896]{1,0:T(8,128)(2,1)S(1)} collective-permute-done((bf16[256,896]{1,0:T(8,128)(2,1)S(1)}, bf16[256,896]{1,0:T(8,128)(2,1)S(1)}, u32[]{:S(2)}, u32[]{:S(2)}) %collective-permute-start.9) | collective-permute-done | bytes 458784 | tf_op jit(solution)/shard_map/ppermute | solution.py:25
  72.8 2.7 %collective-permute-start.10 = (bf16[256,896]{1,0:T(8,128)(2,1)S(1)}, bf16[256,896]{1,0:T(8,128)(2,1)S(1)}, u32[]{:S(2)}, u32[]{:S(2)}) collective-permute-start(bf16[256,896]{1,0:T(8,128)(2,1)S(1)} %add_convert_fusion.2), channel_id=1, source_target_pairs={{0,64},{64,0},{128,192},{192,128},{96,160},{160,96},{224,32},{32,2... | collective-permute-start | bytes 1376264 | tf_op jit(solution)/shard_map/ppermute | solution.py:25
  75.5 2.1 %fusion.15 = bf16[896,1024]{1,0:T(8,128)(2,1)S(1)} fusion(bf16[256,1024]{1,0:T(8,128)(2,1)S(1)} %bitcast.32, bf16[256,1024]{1,0:T(8,128)(2,1)S(1)} %bitcast.30, bf16[256,1024]{1,0:T(8,128)(2,1)S(1)} %bitcast.37, bf16[256,1024]{1,0:T(8,128)(2,1)S(1)} %bitcast.39, bf16[256,896]{1,0:T(8,128)(2,1)S(1)} %bitcast.43, ...), kind=kOutput, calls=%fused_computation.23 | convolution fusion | flops 1895694336 | bytes 5767168 | tf_op jit(solution)/shard_map/dot_general | solution.py:115
  77.8 1.5 %collective-permute-start.14 = (bf16[224,1024]{1,0:T(8,128)(2,1)S(1)}, bf16[224,1024]{1,0:T(8,128)(2,1)}, u32[]{:S(2)}, u32[]{:S(2)}) collective-permute-start(bf16[224,1024]{1,0:T(8,128)(2,1)S(1)} %get-tuple-element.10), channel_id=1, source_target_pairs={{0,3},{1,2},{2,1},{3,0},{33,32},{34,35},{35,34},{32,33},{4,7},{5,6... | collective-permute-start | bytes 1376264 | tf_op jit(solution)/shard_map/ppermute | solution.py:25
  79.3 7.6 %collective-permute-done.10 = bf16[256,896]{1,0:T(8,128)(2,1)S(1)} collective-permute-done((bf16[256,896]{1,0:T(8,128)(2,1)S(1)}, bf16[256,896]{1,0:T(8,128)(2,1)S(1)}, u32[]{:S(2)}, u32[]{:S(2)}) %collective-permute-start.10) | collective-permute-done | bytes 458784 | tf_op jit(solution)/shard_map/ppermute | solution.py:25
  86.9 0.9 add_convert_fusion.1
  87.8 4.4 %all-to-all-start = ((bf16[8,32,896]{2,1,0:T(8,128)(2,1)}), bf16[8,32,896]{2,1,0:T(8,128)(2,1)S(1)}, u32[]{:S(2)}, u32[]{:S(2)}) async-start(bf16[8,32,896]{2,1,0:T(8,128)(2,1)} %bitcast.10), calls=%async_computation | async-start | bytes 917504 | tf_op jit(solution)/shard_map/all_to_all | solution.py:111
  92.2 1.2 %add_convert_fusion = bf16[224,1024]{1,0:T(8,128)(2,1)S(1)} fusion(bf16[224,1024]{1,0:T(8,128)(2,1)} %collective-permute-done.15, bf16[896,1024]{1,0:T(8,128)(2,1)S(1)} %fusion.15, s32[]{:T(128)S(6)} %select_n.222), kind=kLoop, calls=%fused_computation.27 | loop fusion | flops 917504 | bytes 1376260 | tf_op jit(solution)/shard_map/convert_element_type | solution.py:72
  93.5 8.8 %collective-permute-done.16 = bf16[224,1024]{1,0:T(8,128)(2,1)S(1)} collective-permute-done((bf16[224,1024]{1,0:T(8,128)(2,1)S(1)}, bf16[224,1024]{1,0:T(8,128)(2,1)S(1)}, u32[]{:S(2)}, u32[]{:S(2)}) %collective-permute-start.16) | collective-permute-done | bytes 458784 | tf_op jit(solution)/shard_map/ppermute | solution.py:25
  102.3 2.0 %multiply_convert_fusion = bf16[224,1024]{1,0:T(8,128)(2,1)} fusion(bf16[224,1024]{1,0:T(8,128)(2,1)S(1)} %collective-permute-done.16, bf16[224,1024]{1,0:T(8,128)(2,1)} %collective-permute-done.14, bf16[896,1024]{1,0:T(8,128)(2,1)S(1)} %fusion.15, s32[]{:T(128)S(6)} %select_n.223), kind=kLoop, calls=%fused_computation.26 | loop fusion | flops 1605632 | bytes 1835012 | tf_op jit(solution)/shard_map/convert_element_type | solution.py:120
  104.4 4.4 %all-to-all-done = bf16[8,32,896]{2,1,0:T(8,128)(2,1)S(1)} async-done(((bf16[8,32,896]{2,1,0:T(8,128)(2,1)}), bf16[8,32,896]{2,1,0:T(8,128)(2,1)S(1)}, u32[]{:S(2)}, u32[]{:S(2)}) %all-to-all-start) | async-done | bytes 458784 | tf_op jit(solution)/shard_map/all_to_all | solution.py:111
  108.9 1.0 reshape.42
  (41 shorter events, 4.5 us)
Async XLA Ops:
  0.6 14.9 %copy-start.1 = (bf16[1,64,1024]{2,1,0:T(8,128)(2,1)S(1)}, bf16[1,64,1024]{2,1,0:T(8,128)(2,1)}, u32[]{:S(2)}) copy-start(bf16[1,64,1024]{2,1,0:T(8,128)(2,1)} %param.3) | copy-start | bytes 393220
  0.6 14.9 %collective-permute-start = (bf16[64,1024]{1,0:T(8,128)(2,1)}, bf16[64,1024]{1,0:T(8,128)(2,1)S(1)}, u32[]{:S(2)}, u32[]{:S(2)}) collective-permute-start(bf16[64,1024]{1,0:T(8,128)(2,1)} %bitcast.44), channel_id=1, source_target_pairs={{0,4},{4,0},{8,12},{12,8},{16,20},{20,16},{24,28},{28,24},{36,40},... | collective-permute-start | bytes 393224 | tf_op jit(solution)/shard_map/ppermute | solution.py:25
  7.1 39.1 %collective-permute-start.5 = (bf16[224,1024]{1,0:T(8,128)(2,1)}, bf16[224,1024]{1,0:T(8,128)(2,1)S(1)}, u32[]{:S(2)}, u32[]{:S(2)}) collective-permute-start(bf16[224,1024]{1,0:T(8,128)(2,1)} %param.5), channel_id=1, source_target_pairs={{0,1},{1,0},{2,3},{3,2},{33,34},{34,33},{35,32},{32,35},{4,5},{5,4... | collective-permute-start | bytes 1376264 | tf_op jit(solution)/shard_map/ppermute | solution.py:25
  11.7 36.0 %all-to-all-start.1 = ((bf16[8,32,896]{2,1,0:T(8,128)(2,1)}), bf16[8,32,896]{2,1,0:T(8,128)(2,1)S(1)}, u32[]{:S(2)}, u32[]{:S(2)}) async-start(bf16[8,32,896]{2,1,0:T(8,128)(2,1)} %copy.10), calls=%async_computation.1 | async-start | bytes 917504 | tf_op jit(solution)/shard_map/all_to_all | solution.py:91
  15.5 30.7 %copy-start = (bf16[224,1024]{1,0:T(8,128)(2,1)S(1)}, bf16[224,1024]{1,0:T(8,128)(2,1)}, u32[]{:S(2)}) copy-start(bf16[224,1024]{1,0:T(8,128)(2,1)} %param.5) | copy-start | bytes 1376260
  15.6 15.1 %collective-permute-start.1 = (bf16[2,64,1024]{2,1,0:T(8,128)(2,1)S(1)}, bf16[2,64,1024]{2,1,0:T(8,128)(2,1)S(1)}, u32[]{:S(2)}, u32[]{:S(2)}) collective-permute-start(bf16[2,64,1024]{2,1,0:T(8,128)(2,1)S(1)} %reverse_select_fusion), channel_id=1, source_target_pairs={{0,28},{4,8},{8,4},{12,16},{16,12},{20,24},{24,20},{28,0},{36,32},... | collective-permute-start | bytes 786440 | tf_op jit(solution)/shard_map/ppermute | solution.py:25
  30.7 6.4 %collective-permute-start.2 = (bf16[2,64,1024]{2,1,0:T(8,128)(2,1)S(1)}, bf16[2,64,1024]{2,1,0:T(8,128)(2,1)S(1)}, u32[]{:S(2)}, u32[]{:S(2)}) collective-permute-start(bf16[2,64,1024]{2,1,0:T(8,128)(2,1)S(1)} %collective-permute-done.1), channel_id=1, source_target_pairs={{0,4},{4,0},{8,12},{12,8},{16,20},{20,16},{24,28},{28,24},{36,40},... | collective-permute-start | bytes 786440 | tf_op jit(solution)/shard_map/ppermute | solution.py:25
  37.1 5.2 %collective-permute-start.3 = (bf16[2,64,1024]{2,1,0:T(8,128)(2,1)S(1)}, bf16[2,64,1024]{2,1,0:T(8,128)(2,1)S(1)}, u32[]{:S(2)}, u32[]{:S(2)}) collective-permute-start(bf16[2,64,1024]{2,1,0:T(8,128)(2,1)S(1)} %collective-permute-done.2), channel_id=1, source_target_pairs={{0,28},{4,8},{8,4},{12,16},{16,12},{20,24},{24,20},{28,0},{36,32},... | collective-permute-start | bytes 786440 | tf_op jit(solution)/shard_map/ppermute | solution.py:25
  42.4 19.0 %collective-permute-start.4 = (bf16[8,64,1024]{2,1,0:T(8,128)(2,1)S(1)}, bf16[8,64,1024]{2,1,0:T(8,128)(2,1)S(1)}, u32[]{:S(2)}, u32[]{:S(2)}) collective-permute-start(bf16[8,64,1024]{2,1,0:T(8,128)(2,1)S(1)} %slice_dynamic-update-slice_fusion), channel_id=1, source_target_pairs={{0,32},{32,0},{1,33},{33,1},{2,34},{34,2},{3,35},{35,3},{4,36},{36... | collective-permute-start | bytes 3145736 | tf_op jit(solution)/shard_map/ppermute | solution.py:13
  46.2 7.7 %collective-permute-start.6 = (bf16[224,1024]{1,0:T(8,128)(2,1)S(1)}, bf16[224,1024]{1,0:T(8,128)(2,1)}, u32[]{:S(2)}, u32[]{:S(2)}) collective-permute-start(bf16[224,1024]{1,0:T(8,128)(2,1)S(1)} %collective-permute-done.5), channel_id=1, source_target_pairs={{0,3},{1,2},{2,1},{3,0},{33,32},{34,35},{35,34},{32,33},{4,7},{5,6... | collective-permute-start | bytes 1376264 | tf_op jit(solution)/shard_map/ppermute | solution.py:25
  46.2 12.6 %collective-permute-start.7 = (bf16[224,1024]{1,0:T(8,128)(2,1)S(1)}, bf16[224,1024]{1,0:T(8,128)(2,1)}, u32[]{:S(2)}, u32[]{:S(2)}) collective-permute-start(bf16[224,1024]{1,0:T(8,128)(2,1)S(1)} %copy-done), channel_id=1, source_target_pairs={{0,3},{1,2},{2,1},{3,0},{33,32},{34,35},{35,34},{32,33},{4,7},{5,6... | collective-permute-start | bytes 1376264 | tf_op jit(solution)/shard_map/ppermute | solution.py:25
  47.7 12.3 %collective-permute-start.11 = (bf16[256,896]{1,0:T(8,128)(2,1)S(1)}, bf16[256,896]{1,0:T(8,128)(2,1)S(1)}, u32[]{:S(2)}, u32[]{:S(2)}) collective-permute-start(bf16[256,896]{1,0:T(8,128)(2,1)S(1)} %bitcast.41), channel_id=1, source_target_pairs={{0,64},{64,0},{128,192},{192,128},{96,160},{160,96},{224,32},{32,2... | collective-permute-start | bytes 1376264 | tf_op jit(solution)/shard_map/ppermute | solution.py:25
  50.2 25.3 %collective-permute-start.13 = (bf16[256,896]{1,0:T(8,128)(2,1)S(1)}, bf16[256,896]{1,0:T(8,128)(2,1)S(1)}, u32[]{:S(2)}, u32[]{:S(2)}) collective-permute-start(bf16[256,896]{1,0:T(8,128)(2,1)S(1)} %bitcast.42), channel_id=1, source_target_pairs={{0,192},{64,128},{128,64},{192,0},{96,32},{160,224},{224,160},{32,... | collective-permute-start | bytes 1376264 | tf_op jit(solution)/shard_map/ppermute | solution.py:25
  60.1 15.5 %collective-permute-start.12 = (bf16[256,896]{1,0:T(8,128)(2,1)S(1)}, bf16[256,896]{1,0:T(8,128)(2,1)S(1)}, u32[]{:S(2)}, u32[]{:S(2)}) collective-permute-start(bf16[256,896]{1,0:T(8,128)(2,1)S(1)} %collective-permute-done.11), channel_id=1, source_target_pairs={{0,192},{64,128},{128,64},{192,0},{96,32},{160,224},{224,160},{32,... | collective-permute-start | bytes 1376264 | tf_op jit(solution)/shard_map/ppermute | solution.py:25
  63.6 9.1 %collective-permute-start.9 = (bf16[256,896]{1,0:T(8,128)(2,1)S(1)}, bf16[256,896]{1,0:T(8,128)(2,1)S(1)}, u32[]{:S(2)}, u32[]{:S(2)}) collective-permute-start(bf16[256,896]{1,0:T(8,128)(2,1)S(1)} %convolution_convert_fusion), channel_id=1, source_target_pairs={{0,192},{64,128},{128,64},{192,0},{96,32},{160,224},{224,160},{32,... | collective-permute-start | bytes 1376264 | tf_op jit(solution)/shard_map/ppermute | solution.py:25
  65.5 13.8 %collective-permute-start.8 = (bf16[256,896]{1,0:T(8,128)(2,1)S(1)}, bf16[256,896]{1,0:T(8,128)(2,1)S(1)}, u32[]{:S(2)}, u32[]{:S(2)}) collective-permute-start(bf16[256,896]{1,0:T(8,128)(2,1)S(1)} %convolution_convert_fusion.1), channel_id=1, source_target_pairs={{0,192},{64,128},{128,64},{192,0},{96,32},{160,224},{224,160},{32,... | collective-permute-start | bytes 1376264 | tf_op jit(solution)/shard_map/ppermute | solution.py:25
  72.8 14.1 %collective-permute-start.10 = (bf16[256,896]{1,0:T(8,128)(2,1)S(1)}, bf16[256,896]{1,0:T(8,128)(2,1)S(1)}, u32[]{:S(2)}, u32[]{:S(2)}) collective-permute-start(bf16[256,896]{1,0:T(8,128)(2,1)S(1)} %add_convert_fusion.2), channel_id=1, source_target_pairs={{0,64},{64,0},{128,192},{192,128},{96,160},{160,96},{224,32},{32,2... | collective-permute-start | bytes 1376264 | tf_op jit(solution)/shard_map/ppermute | solution.py:25
  77.7 14.5 %collective-permute-start.15 = (bf16[224,1024]{1,0:T(8,128)(2,1)S(1)}, bf16[224,1024]{1,0:T(8,128)(2,1)}, u32[]{:S(2)}, u32[]{:S(2)}) collective-permute-start(bf16[224,1024]{1,0:T(8,128)(2,1)S(1)} %get-tuple-element.11), channel_id=1, source_target_pairs={{0,3},{1,2},{2,1},{3,0},{33,32},{34,35},{35,34},{32,33},{4,7},{5,6... | collective-permute-start | bytes 1376264 | tf_op jit(solution)/shard_map/ppermute | solution.py:25
  77.8 15.7 %collective-permute-start.14 = (bf16[224,1024]{1,0:T(8,128)(2,1)S(1)}, bf16[224,1024]{1,0:T(8,128)(2,1)}, u32[]{:S(2)}, u32[]{:S(2)}) collective-permute-start(bf16[224,1024]{1,0:T(8,128)(2,1)S(1)} %get-tuple-element.10), channel_id=1, source_target_pairs={{0,3},{1,2},{2,1},{3,0},{33,32},{34,35},{35,34},{32,33},{4,7},{5,6... | collective-permute-start | bytes 1376264 | tf_op jit(solution)/shard_map/ppermute | solution.py:25
  87.8 21.0 %all-to-all-start = ((bf16[8,32,896]{2,1,0:T(8,128)(2,1)}), bf16[8,32,896]{2,1,0:T(8,128)(2,1)S(1)}, u32[]{:S(2)}, u32[]{:S(2)}) async-start(bf16[8,32,896]{2,1,0:T(8,128)(2,1)} %bitcast.10), calls=%async_computation | async-start | bytes 917504 | tf_op jit(solution)/shard_map/all_to_all | solution.py:111
  93.4 8.9 %collective-permute-start.16 = (bf16[224,1024]{1,0:T(8,128)(2,1)S(1)}, bf16[224,1024]{1,0:T(8,128)(2,1)S(1)}, u32[]{:S(2)}, u32[]{:S(2)}) collective-permute-start(bf16[224,1024]{1,0:T(8,128)(2,1)S(1)} %add_convert_fusion), channel_id=1, source_target_pairs={{0,1},{1,0},{2,3},{3,2},{33,34},{34,33},{35,32},{32,35},{4,5},{5,4... | collective-permute-start | bytes 1376264 | tf_op jit(solution)/shard_map/ppermute | solution.py:25
